TPU v7x, 512 devices: a whole 4x8x8 slice. The times are simulated.
512 devices in a mesh: inter: 64 (over y, z_hi, core), intra: 8 (over x, z_lo).
Axes of the slice: x: 4, y: 8, z: 8 (z_hi: 4, z_lo: 2; z = z_hi * 2 + z_lo), core: 2. Of those that a mesh axis runs over, the one named last changes fastest.
Arguments:
- hidden_in: bfloat16 [64, 1024, 4096], P('inter', 'intra'), may hold values from -120 to 120, as said below
- norm_gain: bfloat16 [4096], P(('inter', 'intra')), may hold values from 0.5 to 2, as said below
- qkv_weight: bfloat16 [4096, 768], P(('inter', 'intra')), may hold values from -0.09375 to 0.09375
- attn_cotangent: bfloat16 [64, 1024, 512], P('inter', 'intra'), may hold values from -6 to 6
Outputs:
- attn: bfloat16 [64, 1024, 512], P('inter', 'intra')
- grad_in: bfloat16 [64, 1024, 4096], P('inter', 'intra')
- weight_grad: float32 [4096, 768], P(('intra', 'inter'))
- gain_grad: float32 [4096], P(('intra', 'inter'))
Inputs may be any that keep to these rules, and one draw needn't show every extreme that they name: `hidden_in`: activations with spread row and feature scales. `norm_gain`: positive gains.
All inputs are finite; a program needn't handle non-finite values.
Results may differ from a plain program's by a relative error of at most 0.015.
Values may be sent and summed in bfloat16 or wider, within the bound.
A program may use at most 64 MiB of HBM per device.

v0:
```python
import math
import jax
import jax.numpy as jnp
from jax import lax
from jax.sharding import PartitionSpec as P

HD = 128
HEADS = 4
eps_norm = 1e-05
rope_base = 500000.0


def sent_together(arrays, axis, dim, along):
    widths = [math.prod(a.shape[along:]) for a in arrays]
    both = jnp.concatenate(
        [a.reshape(*a.shape[:along], w) for a, w in zip(arrays, widths)], axis=along
    )
    filled = lax.all_gather(both, axis, axis=dim, tiled=True)
    tiles = jnp.split(filled, [sum(widths[:k]) for k in range(1, len(widths))], axis=along)
    return tuple(
        (b.reshape(*filled.shape[:along], *a.shape[along:]) for a, b in zip(arrays, tiles))
    )


def in_one_piece(arrays, axis, dim, along):
    ends, at = ([], 0)
    for a in arrays[:-1]:
        at += a.shape[along]
        ends.append(at)
    both = jnp.concatenate(arrays, axis=along)
    return tuple(jnp.split(lax.all_gather(both, axis, axis=dim, tiled=True), ends, axis=along))


def gather_turned(arrays, axis, dims):
    turned = [jnp.moveaxis(a, dim, 0) for a, dim in zip(arrays, dims)]
    both = jnp.concatenate([t.reshape(len(t), -1) for t in turned], axis=1)
    filled, at, outs = (lax.all_gather(both, axis, axis=0, tiled=True), 0, [])
    for t, dim in zip(turned, dims):
        section = filled[:, at : at + t[0].size].reshape(-1, *t.shape[1:])
        outs.append(jnp.moveaxis(section, 0, dim))
        at += t[0].size
    return tuple(outs)


def in_order(tiles, dim):
    tiles = jnp.moveaxis(tiles, 0, dim)
    dims = tiles.shape
    return tiles.reshape(*dims[:dim], dims[dim] * dims[dim + 1], *dims[dim + 2 :])


def from_everyone(x, axis):
    copies = jnp.broadcast_to(x, (lax.axis_size(axis), *x.shape))
    return lax.all_to_all(copies, axis, split_axis=0, concat_axis=0, tiled=True)


def gather_directly(x, axis, dim):
    return in_order(from_everyone(x, axis), dim)


def split_up(x, dim, size):
    dims = x.shape
    tiles = x.reshape(*dims[:dim], size, dims[dim] // size, *dims[dim + 1 :])
    return jnp.moveaxis(tiles, dim, 0)


def summed_on_arrival(x, axis, dim):
    tiles = split_up(x, dim, lax.axis_size(axis))
    arrived = lax.all_to_all(tiles, axis, split_axis=0, concat_axis=0, tiled=True)
    return arrived.sum(axis=0)


def summed_on_arrival_2(x, axis, dim):
    size = lax.axis_size(axis)
    tiles = lax.all_to_all(split_up(x, dim, size), axis, 0, 0, tiled=True)
    return jnp.sum(tiles.astype(jnp.float32), axis=0)


def side_by_side(arrays, axis, dim, along):
    columns = [a.reshape(*a.shape[:along], -1) for a in arrays]
    both = jnp.concatenate(columns, axis=along)
    filled, at, outs = (summed_on_arrival_2(both, axis, dim), 0, [])
    for a, column in zip(arrays, columns):
        section = filled[..., at : at + column.shape[along]]
        outs.append(section.reshape(*section.shape[:along], *a.shape[along:]))
        at += column.shape[along]
    return tuple(outs)


def rope_tables(positions, head_size):
    half_size = head_size // 2
    freqs = rope_base ** (-jnp.arange(half_size, dtype=jnp.float32) / half_size)
    angles = positions.astype(jnp.float32)[:, None] * freqs[None, :]
    return (jnp.cos(angles), jnp.sin(angles))


def rotate(values_in, cosine, sine):
    half_size = values_in.shape[-1] // 2
    first, second = (values_in[..., :half_size], values_in[..., half_size:])
    return jnp.concatenate(
        [first * cosine - second * sine, second * cosine + first * sine], axis=-1
    )


def unrotate(grad_out, cosine, sine):
    half_size = grad_out.shape[-1] // 2
    first, second = (grad_out[..., :half_size], grad_out[..., half_size:])
    return jnp.concatenate(
        [first * cosine + second * sine, second * cosine - first * sine], axis=-1
    )


def forward_fold(query_rows, row_pos):

    def forward_advance(carry, piece, start):
        row_top, row_total, weighted = carry
        key_part, value_part = piece
        scores = jnp.einsum("qd,kd->qk", query_rows, key_part, preferred_element_type=jnp.float32)
        key_pos = start + jnp.arange(key_part.shape[0], dtype=jnp.int32)
        allowed = key_pos[None, :] <= row_pos[:, None]
        scores = jnp.where(allowed, scores, -1e30)
        new_top = jnp.maximum(row_top, jnp.max(scores, axis=1))
        numbers = jnp.where(allowed, jnp.exp(scores - new_top[:, None]), 0.0)
        row_total = jnp.sum(numbers, axis=1)
        weighted = jnp.dot(
            numbers,
            value_part.astype(jnp.float32),
            precision=lax.Precision.HIGHEST,
            preferred_element_type=jnp.float32,
        )
        return (new_top, row_total, weighted)

    return forward_advance


def query_grad_fold(query_rows, row_pos, grad_flat, log_total, row_delta):

    def query_advance(grad_query, piece, start):
        key_part, value_part = piece
        scores = jnp.einsum("qd,kd->qk", query_rows, key_part, preferred_element_type=jnp.float32)
        key_pos = start + jnp.arange(key_part.shape[0], dtype=jnp.int32)
        allowed = key_pos[None, :] <= row_pos[:, None]
        probs = jnp.where(
            allowed, jnp.exp(jnp.where(allowed, scores, -1e30) - log_total[:, None]), 0.0
        )
        grad_probs = jnp.einsum(
            "qd,kd->qk", grad_flat, value_part, preferred_element_type=jnp.float32
        )
        grad_scores = (probs * (grad_probs - row_delta[:, None])).astype(jnp.bfloat16)
        return jnp.dot(grad_scores, key_part, preferred_element_type=jnp.float32)

    return query_advance


def key_grad_fold(key_rows, value_rows, key_pos, log_all, delta_all, heads_count):

    def key_advance(carry, piece, start):
        query_part, attn_grad_part = piece
        count = query_part.shape[0]
        scores = jnp.einsum("qd,kd->qk", query_part, key_rows, preferred_element_type=jnp.float32)
        query_pos = jnp.arange(count, dtype=jnp.int32) // heads_count
        allowed = key_pos[None, :] <= query_pos[:, None]
        probs = jnp.where(
            allowed, jnp.exp(jnp.where(allowed, scores, -1e30) - log_all[:, None]), 0.0
        )
        grad_values = jnp.einsum(
            "qk,qd->kd",
            probs.astype(jnp.bfloat16),
            attn_grad_part,
            preferred_element_type=jnp.float32,
        )
        grad_probs = jnp.einsum(
            "qd,kd->qk", attn_grad_part, value_rows, preferred_element_type=jnp.float32
        )
        grad_scores = (probs * (grad_probs - delta_all[:, None])).astype(jnp.bfloat16)
        grad_keys = jnp.einsum(
            "qk,qd->kd", grad_scores, query_part, preferred_element_type=jnp.float32
        )
        return (grad_keys, grad_values)

    return key_advance


def local(hidden_in, norm_gain, qkv_weight, attn_cotangent):
    rows_in = hidden_in[0]
    grad_attn = attn_cotangent[0]
    tokens_here = rows_in.shape[0]
    width = rows_in.shape[1]
    head_size = HD
    heads_count = HEADS
    qcols = heads_count * head_size
    scale = head_size ** (-0.5)
    weight_group, gain_group = sent_together((qkv_weight, norm_gain), "intra", 0, 1)
    weight_full, gain_full = sent_together((weight_group, gain_group), "inter", 0, 1)
    query_pos = lax.axis_index("intra") * tokens_here + jnp.arange(tokens_here, dtype=jnp.int32)
    row_pos = jnp.broadcast_to(query_pos[:, None], (tokens_here, heads_count)).reshape(
        tokens_here * heads_count
    )
    cosine, sine = rope_tables(query_pos, head_size)
    wide_rows = rows_in.astype(jnp.float32)
    inv_rms = lax.rsqrt(jnp.mean(wide_rows * wide_rows, axis=1, keepdims=True) + eps_norm)
    normed = (wide_rows * inv_rms * gain_full.astype(jnp.float32)[None, :]).astype(jnp.bfloat16)
    mixed = jnp.dot(normed, weight_full, preferred_element_type=jnp.float32)
    query_rows = (
        (
            rotate(
                mixed[:, :qcols].reshape(tokens_here, heads_count, head_size),
                cosine[:, None, :],
                sine[:, None, :],
            )
            * scale
        )
        .astype(jnp.bfloat16)
        .reshape(tokens_here * heads_count, head_size)
    )
    key_rows = rotate(mixed[:, qcols : qcols + head_size], cosine, sine).astype(jnp.bfloat16)
    value_rows = mixed[:, qcols + head_size :].astype(jnp.bfloat16)
    grad_flat = grad_attn.reshape(tokens_here * heads_count, head_size)
    flat_rows = tokens_here * heads_count
    forward_step = forward_fold(query_rows, row_pos)
    start_carry = (
        jnp.full((flat_rows,), -1e30, jnp.float32),
        jnp.zeros((flat_rows,), jnp.float32),
        jnp.zeros((flat_rows, head_size), jnp.float32),
    )
    key_all, value_all = in_one_piece((key_rows, value_rows), "intra", 0, 1)
    row_top, row_total, weighted = forward_step(start_carry, (key_all, value_all), 0)
    attn_flat = (weighted / row_total[:, None]).astype(jnp.bfloat16)
    log_total = row_top + jnp.log(row_total)
    row_delta = jnp.sum(grad_flat.astype(jnp.float32) * attn_flat.astype(jnp.float32), axis=1)
    query_step = query_grad_fold(query_rows, row_pos, grad_flat, log_total, row_delta)
    grad_query = query_step(jnp.zeros((flat_rows, head_size), jnp.float32), (key_all, value_all), 0)
    log_all, delta_all = gather_turned((log_total, row_delta), "intra", (0, 0))
    key_step = key_grad_fold(key_rows, value_rows, query_pos, log_all, delta_all, heads_count)
    grad_keys, grad_values = key_step(
        (
            jnp.zeros((tokens_here, head_size), jnp.float32),
            jnp.zeros((tokens_here, head_size), jnp.float32),
        ),
        in_one_piece((query_rows, grad_flat), "intra", 0, 1),
        jnp.int32(0),
    )
    query_back = (
        unrotate(
            grad_query.reshape(tokens_here, heads_count, head_size),
            cosine[:, None, :],
            sine[:, None, :],
        )
        * scale
    ).reshape(tokens_here, qcols)
    grad_mixed = jnp.concatenate(
        [query_back, unrotate(grad_keys, cosine, sine), grad_values], axis=1
    ).astype(jnp.bfloat16)
    weight_back, gain_back = (weight_full, gain_full)
    gain_wide = gain_back.astype(jnp.float32)[None, :]
    grad_normed = jnp.einsum(
        "tc,dc->td", grad_mixed, weight_back, preferred_element_type=jnp.float32
    )
    inner = jnp.sum(grad_normed * gain_wide * wide_rows, axis=1, keepdims=True)
    grad_rows = (
        gain_wide * grad_normed * inv_rms - wide_rows * inv_rms**3 / width * inner
    ).astype(jnp.bfloat16)
    gain_term = jnp.sum(grad_normed * wide_rows * inv_rms, axis=0)
    normed_cols = lax.all_to_all(normed, "intra", split_axis=1, concat_axis=0, tiled=True)
    group_term = lax.dot_general(
        normed_cols,
        gather_directly(grad_mixed, "intra", 0),
        (((0,), (0,)), ((), ())),
        preferred_element_type=jnp.float32,
    )
    term_low = lax.optimization_barrier(group_term.astype(jnp.bfloat16))
    gain_sums = summed_on_arrival(gain_term, "intra", 0)
    weight_grad, gain_grad = side_by_side(
        (term_low.astype(jnp.float32).astype(jnp.bfloat16), gain_sums.astype(jnp.bfloat16)),
        "inter",
        0,
        1,
    )
    return (attn_flat.reshape(tokens_here, qcols)[None], grad_rows[None], weight_grad, gain_grad)


def solution(mesh):
    return jax.shard_map(
        local,
        mesh=mesh,
        in_specs=(
            P("inter", "intra", None),
            P(("inter", "intra")),
            P(("inter", "intra"), None),
            P("inter", "intra", None),
        ),
        out_specs=(
            P("inter", "intra", None),
            P("inter", "intra", None),
            P(("intra", "inter"), None),
            P(("intra", "inter")),
        ),
        check_vma=False,
    )
```

profile of v0, /device:TPU:16, one launch (start us, length us, event | category | flops | bytes accessed | tf_op | source)
XLA Modules:
  0.0 335.2 jit_solution(8068869801132005356)
XLA Ops:
  7.2 0.8 copy.32
  8.0 0.7 pad_maximum_fusion.4
  8.8 30.7 %all_gather.15 = bf16[64,769]{1,0:T(8,128)(2,1)} all-gather(bf16[8,769]{1,0:T(8,128)(2,1)S(1)} %pad_maximum_fusion.4), channel_id=1, replica_groups=mesh['inter'=64,'intra'=8] {'intra'}, dimensions={0}, use_global_device_ids=true | all-gather | bytes 110736 | tf_op jit(solution)/shard_map/all_gather | solution.py:18
  40.9 1.0 reshape_squeeze.3
  41.9 0.8 copy.34
  42.6 2.6 copy.44
  46.1 96.7 %all-gather.3.cloned.1.call-done = bf16[4096,769]{1,0:T(8,128)(2,1)} async-done(((bf16[64,769]{1,0:T(8,128)(2,1)}), bf16[4096,769]{1,0:T(8,128)(2,1)}) %all-gather.3.cloned.1.call-update) | async-done | bytes 6299664 | tf_op jit(solution)/shard_map/all_gather | solution.py:18
  142.8 1.6 convert_reduce_fusion
  144.4 3.8 %fusion.2 = f32[128,768]{1,0:T(8,128)S(1)} fusion(bf16[4096,769]{1,0:T(8,128)(2,1)} %all-gather.3.cloned.1.call-done, bf16[1,128,4096]{2,1,0:T(8,128)(2,1)S(1)} %copy-done, f32[4096]{0:T(1024)S(1)} %convert_reduce_fusion, f32[128]{0:T(128)S(1)} %get-tuple-element.19), kind=kOutput, calls=%fused_computation.2 | convolution fusion | flops 807403520 | bytes 7750144 | tf_op jit(solution)/shard_map/dot_general | solution.py:202
  149.2 0.7 pad_maximum_fusion.1
  151.3 32.7 %all_gather.17 = bf16[1024,256]{1,0:T(8,128)(2,1)S(1)} all-gather(bf16[128,256]{1,0:T(8,128)(2,1)S(1)} %pad_maximum_fusion.3), channel_id=1, replica_groups=mesh['inter'=64,'intra'=8] {'intra'}, dimensions={0}, use_global_device_ids=true | all-gather | bytes 589824 | tf_op jit(solution)/shard_map/all_gather | solution.py:31
  183.9 1.3 fusion.79
  185.2 1.3 fusion.20
  186.6 2.4 multiply_reduce_fusion
  189.0 2.6 fusion.23
  191.6 1.4 multiply_add_fusion
  193.4 1.5 multiply_convert_fusion
  194.9 4.3 %all-to-all-start = ((bf16[128,8,512]{0,2,1:T(8,128)(2,1)}), bf16[128,8,512]{0,2,1:T(8,128)(2,1)}, u32[]{:S(2)}, u32[]{:S(2)}) async-start(bf16[128,8,512]{0,2,1:T(8,128)(2,1)} %multiply_convert_fusion), calls=%async_computation | async-start | bytes 2097152 | tf_op jit(solution)/shard_map/all_to_all | solution.py:263
  199.2 43.5 %all_gather.19 = f32[4096,2]{0,1:T(2,128)S(1)} all-gather(f32[512,2]{0,1:T(2,128)S(1)} %pad_maximum_fusion.5), channel_id=1, replica_groups=mesh['inter'=64,'intra'=8] {'intra'}, dimensions={0}, use_global_device_ids=true | all-gather | bytes 36864 | tf_op jit(solution)/shard_map/all_gather | solution.py:37
  242.7 3.3 fusion.6
  246.7 3.0 fusion.22
  250.2 6.3 %fusion.18 = (f32[4096]{0:T(1024)S(1)}, f32[128]{0:T(128)S(1)}, f32[128,4096]{1,0:T(8,128)}) fusion(bf16[1,128,4096]{2,1,0:T(8,128)(2,1)S(1)} %copy-done, f32[128]{0:T(128)S(1)} %copy-done.21, f32[4096]{0:T(1024)S(1)} %convert_reduce_fusion, bf16[128,768]{1,0:T(8,128)(2,1)S(1)} %pad_maximum_fusion.2, bf16[4096,769]{1,0:T(8,128)(2,1)} %all-gather.3.cloned.1.call-done), kind=kOutput, calls=%fused_computation.26 | convolution fusion | flops 808972160 | bytes 9667584 | tf_op jit(solution)/shard_map/tc,dc->td/dot_general | solution.py:255
  256.6 8.6 %all_to_all.32 = f32[8,1,512]{2,1,0:T(1,128)S(1)} all-to-all(f32[8,1,512]{2,1,0:T(1,128)S(1)} %bitcast.67), channel_id=1, replica_groups=mesh['inter'=64,'intra'=8] {'intra'}, dimensions={0} | all-to-all | bytes 32768 | tf_op jit(solution)/shard_map/all_to_all | solution.py:68
  265.1 1.3 broadcast_in_dim.59
  266.4 3.6 %all-to-all-start.1 = ((bf16[8,128,768]{2,1,0:T(8,128)(2,1)}), bf16[8,128,768]{2,1,0:T(8,128)(2,1)S(1)}, u32[]{:S(2)}, u32[]{:S(2)}) async-start(bf16[8,128,768]{2,1,0:T(8,128)(2,1)} %broadcast_in_dim.59), calls=%async_computation.1 | async-start | bytes 3145728 | tf_op jit(solution)/shard_map/all_to_all | solution.py:53
  270.3 14.0 %all-to-all-done.1 = bf16[8,128,768]{2,1,0:T(8,128)(2,1)S(1)} async-done(((bf16[8,128,768]{2,1,0:T(8,128)(2,1)}), bf16[8,128,768]{2,1,0:T(8,128)(2,1)S(1)}, u32[]{:S(2)}, u32[]{:S(2)}) %all-to-all-start.1) | async-done | bytes 1572896 | tf_op jit(solution)/shard_map/all_to_all | solution.py:53
  284.3 2.2 bitcast_convert_fusion
  286.5 1.0 pad_maximum_fusion
  287.5 11.4 %all-to-all-start.3 = ((bf16[64,8,769]{2,1,0:T(8,128)(2,1)}), bf16[64,8,769]{2,1,0:T(8,128)(2,1)S(1)}, u32[]{:S(2)}, u32[]{:S(2)}) async-start(bf16[64,8,769]{2,1,0:T(8,128)(2,1)} %pad_maximum_fusion), calls=%async_computation.3 | async-start | bytes 1835008 | tf_op jit(solution)/shard_map/all_to_all | solution.py:74
  299.0 0.7 broadcast_in_dim_reshape.2
  299.8 3.2 fusion.26
  302.9 24.0 %all-to-all-done.3 = bf16[64,8,769]{2,1,0:T(8,128)(2,1)S(1)} async-done(((bf16[64,8,769]{2,1,0:T(8,128)(2,1)}), bf16[64,8,769]{2,1,0:T(8,128)(2,1)S(1)}, u32[]{:S(2)}, u32[]{:S(2)}) %all-to-all-start.3) | async-done | bytes 787488 | tf_op jit(solution)/shard_map/all_to_all | solution.py:74
  (89 shorter events, 7.8 us)
Async XLA Ops:
  7.2 38.1 %copy-start = (bf16[1,128,4096]{2,1,0:T(8,128)(2,1)S(1)}, bf16[1,128,4096]{2,1,0:T(8,128)(2,1)}, u32[]{:S(2)}) copy-start(bf16[1,128,4096]{2,1,0:T(8,128)(2,1)} %param.4) | copy-start | bytes 3145732
  7.2 135.6 %all-gather.3.cloned.1.call-start = ((), (), s32[]{:S(2)}) async-start(), calls=%async_computation.4 | async-start | bytes 7454720 | tf_op jit(solution)/shard_map/all_gather | solution.py:18
  39.5 203.2 %all-gather.5.cloned.1.call-start = ((), (), s32[]{:S(2)}) async-start(), calls=%async_computation.5 | async-start | bytes 2359296 | tf_op jit(solution)/shard_map/all_gather | solution.py:31
  39.5 0.5 copy-start.23
  45.3 103.1 %copy-start.15 = (f32[128]{0:T(128)}, f32[128]{0:T(128)S(1)}, u32[]{:S(2)}) copy-start(f32[128]{0:T(128)S(1)} %fusion.77) | copy-start | bytes 1540
  45.3 103.1 %copy-start.17 = (f32[64]{0:T(128)}, f32[64]{0:T(128)S(1)}, u32[]{:S(2)}) copy-start(f32[64]{0:T(128)S(1)} %multiply_power_fusion) | copy-start | bytes 772
  46.1 102.1 %copy-start.19 = (f32[128]{0:T(128)}, f32[128]{0:T(128)S(1)}, u32[]{:S(2)}) copy-start(f32[128]{0:T(128)S(1)} %get-tuple-element.19) | copy-start | bytes 1540
  148.2 3.0 copy-start.4
  148.7 2.6 copy-start.5
  148.7 2.6 copy-start.7
  183.9 2.6 copy-start.3
  183.9 2.6 copy-start.10
  183.9 2.7 copy-start.12
  186.6 2.4 copy-start.13
  189.0 4.2 %copy-start.11 = (f32[8,512]{1,0:T(8,128)S(1)}, f32[8,512]{1,0:T(8,128)}, u32[]{:S(2)}) copy-start(f32[8,512]{1,0:T(8,128)} %reshape.205) | copy-start | bytes 49156
  191.6 1.7 copy-start.1
  191.6 1.7 copy-start.20
  193.4 49.3 %copy-start.6 = (bf16[128,64]{1,0:T(8,128)(2,1)S(1)}, bf16[128,64]{1,0:T(8,128)(2,1)}, u32[]{:S(2)}) copy-start(bf16[128,64]{1,0:T(8,128)(2,1)} %copy-done.5) | copy-start | bytes 49156
  193.4 49.3 %copy-start.8 = (bf16[128,64]{1,0:T(8,128)(2,1)S(1)}, bf16[128,64]{1,0:T(8,128)(2,1)}, u32[]{:S(2)}) copy-start(bf16[128,64]{1,0:T(8,128)(2,1)} %copy-done.7) | copy-start | bytes 49156
  193.4 49.3 %copy-start.14 = (s32[4096]{0:T(1024)S(1)}, s32[4096]{0:T(1024)}, u32[]{:S(2)}) copy-start(s32[4096]{0:T(1024)} %add_select_fusion) | copy-start | bytes 49156
  193.4 49.3 %copy-start.24 = (s32[128]{0:T(128)S(1)}, s32[128]{0:T(128)}, u32[]{:S(2)}) copy-start(s32[128]{0:T(128)} %copy-done.23) | copy-start | bytes 1540
  194.9 61.7 %all-to-all-start = ((bf16[128,8,512]{0,2,1:T(8,128)(2,1)}), bf16[128,8,512]{0,2,1:T(8,128)(2,1)}, u32[]{:S(2)}, u32[]{:S(2)}) async-start(bf16[128,8,512]{0,2,1:T(8,128)(2,1)} %multiply_convert_fusion), calls=%async_computation | async-start | bytes 2097152 | tf_op jit(solution)/shard_map/all_to_all | solution.py:263
  242.7 3.3 copy-start.2
  246.7 3.1 copy-start.16
  246.7 3.1 copy-start.18
  246.7 3.5 %copy-start.21 = (f32[128]{0:T(128)S(1)}, f32[128]{0:T(128)}, u32[]{:S(2)}) copy-start(f32[128]{0:T(128)} %copy-done.19) | copy-start | bytes 1540
  266.4 17.9 %all-to-all-start.1 = ((bf16[8,128,768]{2,1,0:T(8,128)(2,1)}), bf16[8,128,768]{2,1,0:T(8,128)(2,1)S(1)}, u32[]{:S(2)}, u32[]{:S(2)}) async-start(bf16[8,128,768]{2,1,0:T(8,128)(2,1)} %broadcast_in_dim.59), calls=%async_computation.1 | async-start | bytes 3145728 | tf_op jit(solution)/shard_map/all_to_all | solution.py:53
  286.5 12.4 %copy-start.9 = (bf16[512,128]{0,1:T(8,128)(2,1)S(1)}, bf16[512,128]{0,1:T(8,128)(2,1)}, u32[]{:S(2)}) copy-start(bf16[512,128]{0,1:T(8,128)(2,1)} %get-tuple-element.23) | copy-start | bytes 393220
  286.5 13.3 %copy-start.22 = (f32[128]{0:T(128)S(1)}, f32[128]{0:T(128)}, u32[]{:S(2)}) copy-start(f32[128]{0:T(128)} %get-tuple-element.18) | copy-start | bytes 1540
  287.5 39.5 %all-to-all-start.3 = ((bf16[64,8,769]{2,1,0:T(8,128)(2,1)}), bf16[64,8,769]{2,1,0:T(8,128)(2,1)S(1)}, u32[]{:S(2)}, u32[]{:S(2)}) async-start(bf16[64,8,769]{2,1,0:T(8,128)(2,1)} %pad_maximum_fusion), calls=%async_computation.3 | async-start | bytes 1835008 | tf_op jit(solution)/shard_map/all_to_all | solution.py:74
Sparse Core Ops, SparseCore 0:
  39.6 103.1 all-gather.2
  150.0 67.2 all-gather.4
where the time goes:
time: 336 us; the launch traced here: 335 us
  waiting for transfers between devices  135 us (40%)
  blocking collectives  115 us (34%)
  matrix products  25.5 us (8%)
  starting transfers between devices  19.3 us (6%)
  other arithmetic  14.6 us (4%)
  between operations  14.5 us (4%)
  local copies, waits for them, and re-layouts  11.2 us (3%)
    all_gather x1, waiting for transfers between devices, sent_together(): filled = lax.all_gather(both, axis, axis=dim, tiled=True)  96.7 us
    all_gather x1, blocking collectives, gather_turned(): filled, at, outs = (lax.all_gather(both, axis, axis=0, tiled=True), 0, [])  43.5 us
    all_gather x1, blocking collectives, in_one_piece(): lax.all_gather(both, axis, axis=dim, tiled=True)  32.7 us
    all_gather x1, blocking collectives, sent_together(): filled = lax.all_gather(both, axis, axis=dim, tiled=True)  30.7 us
    all_to_all x1, waiting for transfers between devices, summed_on_arrival_2(): tiles = lax.all_to_all(split_up(x, dim, size), axis, 0, 0, tiled=True)  24 us
    all_to_all x1, waiting for transfers between devices, from_everyone(): return lax.all_to_all(copies, axis, split_axis=0, concat_axis=0, tiled=True)  14 us
    all_to_all x1, starting transfers between devices, summed_on_arrival_2(): tiles = lax.all_to_all(split_up(x, dim, size), axis, 0, 0, tiled=True)  11.4 us
    all_to_all x1, blocking collectives, summed_on_arrival(): lax.all_to_all(tiles, axis, split_axis=0, concat_axis=0, tiled=True)  8.56 us
  transfers between devices with their start and end apart: 5, of which 3 were waited for; matrix products, arithmetic and copies ran while one was open for 11% of the time, Pallas kernels for 0%

commit v1 on v0

--- a/solution.py
+++ b/solution.py
@@ -8,6 +8,11 @@
 HEADS = 4
 eps_norm = 1e-05
 rope_base = 500000.0
+
+
+def swapped_in(shard, name, along):
+    stack = jnp.stack([shard] * lax.axis_size(name))
+    return jnp.concatenate(lax.all_to_all(stack, name, 0, 0), axis=along)
 
 
 def sent_together(arrays, axis, dim, along):
@@ -34,7 +39,7 @@
 def gather_turned(arrays, axis, dims):
     turned = [jnp.moveaxis(a, dim, 0) for a, dim in zip(arrays, dims)]
     both = jnp.concatenate([t.reshape(len(t), -1) for t in turned], axis=1)
-    filled, at, outs = (lax.all_gather(both, axis, axis=0, tiled=True), 0, [])
+    filled, at, outs = (swapped_in(both, axis, 0), 0, [])
     for t, dim in zip(turned, dims):
         section = filled[:, at : at + t[0].size].reshape(-1, *t.shape[1:])
         outs.append(jnp.moveaxis(section, 0, dim))

time: 336 us -> 315 us (0.938)
  blocking collectives: 115 us -> 73.5 us
  waiting for transfers between devices: 135 us -> 145 us
  starting transfers between devices: 19.3 us -> 28 us
    all_gather x1 -> x0, blocking collectives: 43.5 us -> none  [gather_turned(): filled, at, outs = (lax.all_gather(both, axis, axis=0, tiled=True), 0, [])]
    all_to_all x1, waiting for transfers between devices: 14 us -> 19.1 us  [from_everyone(): return lax.all_to_all(copies, axis, split_axis=0, concat_axis=0, tiled=True)]
    all_gather x1, waiting for transfers between devices: 0.02 us -> 4.89 us  [in_one_piece(): lax.all_gather(both, axis, axis=dim, tiled=True)]
    all_to_all x0 -> x1, starting transfers between devices: none -> 3.95 us  [swapped_in(): return jnp.concatenate(lax.all_to_all(stack, name, 0, 0), axis=along)]
    all_to_all x1, starting transfers between devices: 11.4 us -> 14.8 us  [summed_on_arrival_2(): tiles = lax.all_to_all(split_up(x, dim, size), axis, 0, 0, tiled=True)]
  transfers between devices with their start and end apart: 5 -> 6, of which waited for: 3 -> 4; matrix products, arithmetic and copies ran while one was open for 11% -> 12% of each run, Pallas kernels for 0% -> 0%
where the time goes in v1:
time: 315 us; the launch traced here: 314 us
  waiting for transfers between devices  145 us (46%)
  blocking collectives  73.5 us (23%)
  starting transfers between devices  28 us (9%)
  matrix products  25.5 us (8%)
  other arithmetic  15.6 us (5%)
  between operations  14.5 us (5%)
  local copies, waits for them, and re-layouts  12.5 us (4%)
    all_gather x1, waiting for transfers between devices, sent_together(): filled = lax.all_gather(both, axis, axis=dim, tiled=True)  96.7 us
    all_gather x1, blocking collectives, in_one_piece(): lax.all_gather(both, axis, axis=dim, tiled=True)  32.6 us
    all_gather x1, blocking collectives, sent_together(): filled = lax.all_gather(both, axis, axis=dim, tiled=True)  30.7 us
    all_to_all x1, waiting for transfers between devices, summed_on_arrival_2(): tiles = lax.all_to_all(split_up(x, dim, size), axis, 0, 0, tiled=True)  24 us
    all_to_all x1, waiting for transfers between devices, from_everyone(): return lax.all_to_all(copies, axis, split_axis=0, concat_axis=0, tiled=True)  19.1 us
    all_to_all x1, starting transfers between devices, summed_on_arrival_2(): tiles = lax.all_to_all(split_up(x, dim, size), axis, 0, 0, tiled=True)  14.8 us
    all_to_all x1, blocking collectives, summed_on_arrival(): lax.all_to_all(tiles, axis, split_axis=0, concat_axis=0, tiled=True)  10.1 us
    dot_general x1, matrix products, local(): jnp.einsum('tc,dc->td', grad_mixed, weight_back, preferred_element_type=j...  6.4 us
  transfers between devices with their start and end apart: 6, of which 4 were waited for; matrix products, arithmetic and copies ran while one was open for 12% of the time, Pallas kernels for 0%

profile of v1, /device:TPU:16, one launch (start us, length us, event | category | flops | bytes accessed | tf_op | source)
XLA Modules:
  0.0 314.4 jit_solution(15494267730667985198)
XLA Ops:
  7.2 0.8 copy.41
  8.8 30.7 %all_gather.12 = bf16[64,769]{1,0:T(8,128)(2,1)} all-gather(bf16[8,769]{1,0:T(8,128)(2,1)S(1)} %pad_maximum_fusion.4), channel_id=1, replica_groups=mesh['inter'=64,'intra'=8] {'intra'}, dimensions={0}, use_global_device_ids=true | all-gather | bytes 110736 | tf_op jit(solution)/shard_map/all_gather | solution.py:23
  40.9 1.0 reshape_squeeze.3
  41.9 0.8 copy.43
  42.6 2.6 copy.53
  46.1 96.7 %all-gather.3.cloned.1.call-done = bf16[4096,769]{1,0:T(8,128)(2,1)} async-done(((bf16[64,769]{1,0:T(8,128)(2,1)}), bf16[4096,769]{1,0:T(8,128)(2,1)}) %all-gather.3.cloned.1.call-update) | async-done | bytes 6299664 | tf_op jit(solution)/shard_map/all_gather | solution.py:23
  142.8 1.6 convert_reduce_fusion
  144.4 3.8 %fusion.2 = f32[128,768]{1,0:T(8,128)S(1)} fusion(bf16[4096,769]{1,0:T(8,128)(2,1)} %all-gather.3.cloned.1.call-done, bf16[1,128,4096]{2,1,0:T(8,128)(2,1)S(1)} %copy-done, f32[4096]{0:T(1024)S(1)} %convert_reduce_fusion, f32[128]{0:T(128)S(1)} %get-tuple-element.19), kind=kOutput, calls=%fused_computation.2 | convolution fusion | flops 807403520 | bytes 7750144 | tf_op jit(solution)/shard_map/dot_general | solution.py:207
  151.2 32.6 %all_gather.14 = bf16[1024,256]{1,0:T(8,128)(2,1)S(1)} all-gather(bf16[128,256]{1,0:T(8,128)(2,1)S(1)} %pad_maximum_fusion.3), channel_id=1, replica_groups=mesh['inter'=64,'intra'=8] {'intra'}, dimensions={0}, use_global_device_ids=true | all-gather | bytes 589824 | tf_op jit(solution)/shard_map/all_gather | solution.py:36
  183.9 1.2 fusion.79
  185.1 1.3 fusion.20
  186.4 2.4 multiply_reduce_fusion
  189.5 4.0 %all-to-all-start = ((f32[8,512,2]{1,2,0:T(2,128)}), f32[8,512,2]{1,2,0:T(2,128)}, u32[]{:S(2)}, u32[]{:S(2)}) async-start(f32[8,512,2]{1,2,0:T(2,128)} %stack.2), calls=%async_computation | async-start | bytes 65536 | tf_op jit(solution)/shard_map/all_to_all | solution.py:15
  193.5 2.6 fusion.23
  196.0 1.3 multiply_add_fusion
  197.4 2.7 multiply_convert_fusion
  200.3 5.6 %all-to-all-start.1 = ((bf16[128,8,512]{0,2,1:T(8,128)(2,1)}), bf16[128,8,512]{0,2,1:T(8,128)(2,1)}, u32[]{:S(2)}, u32[]{:S(2)}) async-start(bf16[128,8,512]{0,2,1:T(8,128)(2,1)} %multiply_convert_fusion), calls=%async_computation.1 | async-start | bytes 2097152 | tf_op jit(solution)/shard_map/all_to_all | solution.py:268
  206.0 0.9 fusion.78
  206.8 4.9 %all-gather.5.cloned.1.call-done = bf16[4096,256]{1,0:T(8,128)(2,1)} async-done(((bf16[512,256]{1,0:T(8,128)(2,1)}), bf16[4096,256]{1,0:T(8,128)(2,1)}) %all-gather.5.cloned.1.call-update) | async-done | bytes 2097168 | tf_op jit(solution)/shard_map/all_gather | solution.py:36
  211.7 3.3 %fusion.6 = f32[4096,128]{1,0:T(8,128)S(1)} fusion(f32[4096]{0:T(1024)S(1)} %bitcast.69, s32[128]{0:T(128)S(1)} %copy-done.23, s32[4096]{0:T(1024)S(1)} %copy-done.13, bf16[4096,256]{1,0:T(8,128)(2,1)} %all-gather.5.cloned.1.call-done, bf16[128,64]{1,0:T(8,128)(2,1)S(1)} %copy-done.7, bf16[128,64]{1,0:T(8,128)(2,1)S(1)} %copy-done.5), kind=kOutput, calls=%fused_computation.7 | convolution fusion | flops 136380416 | bytes 3211776 | tf_op jit(solution)/shard_map/qd,kd->qk/dot_general | solution.py:164
  215.7 3.0 fusion.22
  219.2 6.4 %fusion.18 = (f32[4096]{0:T(1024)S(1)}, f32[128]{0:T(128)S(1)}, f32[128,4096]{1,0:T(8,128)}) fusion(bf16[1,128,4096]{2,1,0:T(8,128)(2,1)S(1)} %copy-done, f32[128]{0:T(128)S(1)} %copy-done.20, f32[4096]{0:T(1024)S(1)} %convert_reduce_fusion, bf16[128,768]{1,0:T(8,128)(2,1)S(1)} %pad_maximum_fusion.2, bf16[4096,769]{1,0:T(8,128)(2,1)} %all-gather.3.cloned.1.call-done), kind=kOutput, calls=%fused_computation.26 | convolution fusion | flops 808972160 | bytes 9667584 | tf_op jit(solution)/shard_map/tc,dc->td/dot_general | solution.py:260
  225.6 10.1 %all_to_all.37 = f32[8,1,512]{2,1,0:T(1,128)S(1)} all-to-all(f32[8,1,512]{2,1,0:T(1,128)S(1)} %bitcast.68), channel_id=1, replica_groups=mesh['inter'=64,'intra'=8] {'intra'}, dimensions={0} | all-to-all | bytes 32768 | tf_op jit(solution)/shard_map/all_to_all | solution.py:73
  235.8 1.3 broadcast_in_dim.59
  237.0 3.6 %all-to-all-start.2 = ((bf16[8,128,768]{2,1,0:T(8,128)(2,1)}), bf16[8,128,768]{2,1,0:T(8,128)(2,1)S(1)}, u32[]{:S(2)}, u32[]{:S(2)}) async-start(bf16[8,128,768]{2,1,0:T(8,128)(2,1)} %broadcast_in_dim.59), calls=%async_computation.2 | async-start | bytes 3145728 | tf_op jit(solution)/shard_map/all_to_all | solution.py:58
  240.9 19.1 %all-to-all-done.2 = bf16[8,128,768]{2,1,0:T(8,128)(2,1)S(1)} async-done(((bf16[8,128,768]{2,1,0:T(8,128)(2,1)}), bf16[8,128,768]{2,1,0:T(8,128)(2,1)S(1)}, u32[]{:S(2)}, u32[]{:S(2)}) %all-to-all-start.2) | async-done | bytes 1572896 | tf_op jit(solution)/shard_map/all_to_all | solution.py:58
  260.0 2.2 bitcast_convert_fusion
  262.2 1.0 pad_maximum_fusion
  263.2 14.8 %all-to-all-start.4 = ((bf16[64,8,769]{2,1,0:T(8,128)(2,1)}), bf16[64,8,769]{2,1,0:T(8,128)(2,1)S(1)}, u32[]{:S(2)}, u32[]{:S(2)}) async-start(bf16[64,8,769]{2,1,0:T(8,128)(2,1)} %pad_maximum_fusion), calls=%async_computation.4 | async-start | bytes 1835008 | tf_op jit(solution)/shard_map/all_to_all | solution.py:79
  278.1 0.7 broadcast_in_dim_reshape.2
  278.9 3.2 %fusion.26 = bf16[1,128,4096]{2,1,0:T(8,128)(2,1)} fusion(bf16[1,128,4096]{2,1,0:T(8,128)(2,1)S(1)} %copy-done, f32[128,4096]{1,0:T(8,128)} %get-tuple-element.24, f32[128]{0:T(128)S(1)} %broadcast_multiply_fusion, f32[128]{0:T(128)S(1)} %copy-done.21, f32[4096]{0:T(1024)S(1)} %convert_reduce_fusion, f32[128]{0:T(128)S(1)} %copy-done.20), kind=kLoop, calls=%fused_computation.41 | loop fusion | flops 3670016 | bytes 4212224 | tf_op jit(solution)/shard_map/broadcast_in_dim | solution.py:283
  282.1 24.0 %all-to-all-done.4 = bf16[64,8,769]{2,1,0:T(8,128)(2,1)S(1)} async-done(((bf16[64,8,769]{2,1,0:T(8,128)(2,1)}), bf16[64,8,769]{2,1,0:T(8,128)(2,1)S(1)}, u32[]{:S(2)}, u32[]{:S(2)}) %all-to-all-start.4) | async-done | bytes 787488 | tf_op jit(solution)/shard_map/all_to_all | solution.py:79
  (89 shorter events, 9.7 us)
Async XLA Ops:
  7.2 38.1 %copy-start = (bf16[1,128,4096]{2,1,0:T(8,128)(2,1)S(1)}, bf16[1,128,4096]{2,1,0:T(8,128)(2,1)}, u32[]{:S(2)}) copy-start(bf16[1,128,4096]{2,1,0:T(8,128)(2,1)} %param.4) | copy-start | bytes 3145732
  7.2 135.6 %all-gather.3.cloned.1.call-start = ((), (), s32[]{:S(2)}) async-start(), calls=%async_computation.5 | async-start | bytes 7454720 | tf_op jit(solution)/shard_map/all_gather | solution.py:23
  39.5 172.2 %all-gather.5.cloned.1.call-start = ((), (), s32[]{:S(2)}) async-start(), calls=%async_computation.6 | async-start | bytes 2359296 | tf_op jit(solution)/shard_map/all_gather | solution.py:36
  39.5 0.6 copy-start.22
  45.2 103.1 %copy-start.14 = (f32[128]{0:T(128)}, f32[128]{0:T(128)S(1)}, u32[]{:S(2)}) copy-start(f32[128]{0:T(128)S(1)} %fusion.77) | copy-start | bytes 1540
  45.2 103.1 %copy-start.16 = (f32[64]{0:T(128)}, f32[64]{0:T(128)S(1)}, u32[]{:S(2)}) copy-start(f32[64]{0:T(128)S(1)} %multiply_power_fusion) | copy-start | bytes 772
  46.1 102.1 %copy-start.18 = (f32[128]{0:T(128)}, f32[128]{0:T(128)S(1)}, u32[]{:S(2)}) copy-start(f32[128]{0:T(128)S(1)} %get-tuple-element.19) | copy-start | bytes 1540
  148.2 3.0 copy-start.3
  148.7 2.5 copy-start.4
  148.7 2.5 copy-start.6
  183.9 2.5 copy-start.2
  183.9 2.5 copy-start.9
  183.9 2.5 copy-start.11
  186.4 7.0 %copy-start.12 = (s32[512]{0:T(512)S(1)}, s32[512]{0:T(512)}, u32[]{:S(2)}) copy-start(s32[512]{0:T(512)} %le.15) | copy-start | bytes 6148
  189.5 10.9 %all-to-all-start = ((f32[8,512,2]{1,2,0:T(2,128)}), f32[8,512,2]{1,2,0:T(2,128)}, u32[]{:S(2)}, u32[]{:S(2)}) async-start(f32[8,512,2]{1,2,0:T(2,128)} %stack.2), calls=%async_computation | async-start | bytes 65536 | tf_op jit(solution)/shard_map/all_to_all | solution.py:15
  193.4 3.9 %copy-start.10 = (f32[8,512]{1,0:T(8,128)S(1)}, f32[8,512]{1,0:T(8,128)}, u32[]{:S(2)}) copy-start(f32[8,512]{1,0:T(8,128)} %reshape.211) | copy-start | bytes 49156
  193.5 3.9 %copy-start.19 = (f32[128]{0:T(128)S(1)}, f32[128]{0:T(128)}, u32[]{:S(2)}) copy-start(f32[128]{0:T(128)} %copy-done.18) | copy-start | bytes 1540
  200.1 11.6 %copy-start.5 = (bf16[128,64]{1,0:T(8,128)(2,1)S(1)}, bf16[128,64]{1,0:T(8,128)(2,1)}, u32[]{:S(2)}) copy-start(bf16[128,64]{1,0:T(8,128)(2,1)} %copy-done.4) | copy-start | bytes 49156
  200.1 11.6 %copy-start.7 = (bf16[128,64]{1,0:T(8,128)(2,1)S(1)}, bf16[128,64]{1,0:T(8,128)(2,1)}, u32[]{:S(2)}) copy-start(bf16[128,64]{1,0:T(8,128)(2,1)} %copy-done.6) | copy-start | bytes 49156
  200.1 11.6 %copy-start.13 = (s32[4096]{0:T(1024)S(1)}, s32[4096]{0:T(1024)}, u32[]{:S(2)}) copy-start(s32[4096]{0:T(1024)} %add_select_fusion) | copy-start | bytes 49156
  200.1 11.6 %copy-start.23 = (s32[128]{0:T(128)S(1)}, s32[128]{0:T(128)}, u32[]{:S(2)}) copy-start(s32[128]{0:T(128)} %copy-done.22) | copy-start | bytes 1540
  200.3 25.3 %all-to-all-start.1 = ((bf16[128,8,512]{0,2,1:T(8,128)(2,1)}), bf16[128,8,512]{0,2,1:T(8,128)(2,1)}, u32[]{:S(2)}, u32[]{:S(2)}) async-start(bf16[128,8,512]{0,2,1:T(8,128)(2,1)} %multiply_convert_fusion), calls=%async_computation.1 | async-start | bytes 2097152 | tf_op jit(solution)/shard_map/all_to_all | solution.py:268
  211.7 3.3 %copy-start.1 = (bf16[4096,256]{1,0:T(8,128)(2,1)S(1)}, bf16[4096,256]{1,0:T(8,128)(2,1)}, u32[]{:S(2)}) copy-start(bf16[4096,256]{1,0:T(8,128)(2,1)} %all-gather.5.cloned.1.call-done) | copy-start | bytes 6291460
  215.7 3.1 copy-start.15
  215.7 3.1 copy-start.17
  215.7 3.5 %copy-start.20 = (f32[128]{0:T(128)S(1)}, f32[128]{0:T(128)}, u32[]{:S(2)}) copy-start(f32[128]{0:T(128)} %copy-done.18) | copy-start | bytes 1540
  237.0 23.0 %all-to-all-start.2 = ((bf16[8,128,768]{2,1,0:T(8,128)(2,1)}), bf16[8,128,768]{2,1,0:T(8,128)(2,1)S(1)}, u32[]{:S(2)}, u32[]{:S(2)}) async-start(bf16[8,128,768]{2,1,0:T(8,128)(2,1)} %broadcast_in_dim.59), calls=%async_computation.2 | async-start | bytes 3145728 | tf_op jit(solution)/shard_map/all_to_all | solution.py:58
  262.2 15.8 %copy-start.8 = (bf16[512,128]{0,1:T(8,128)(2,1)S(1)}, bf16[512,128]{0,1:T(8,128)(2,1)}, u32[]{:S(2)}) copy-start(bf16[512,128]{0,1:T(8,128)(2,1)} %get-tuple-element.23) | copy-start | bytes 393220
  262.2 16.6 %copy-start.21 = (f32[128]{0:T(128)S(1)}, f32[128]{0:T(128)}, u32[]{:S(2)}) copy-start(f32[128]{0:T(128)} %get-tuple-element.18) | copy-start | bytes 1540
  263.2 42.9 %all-to-all-start.4 = ((bf16[64,8,769]{2,1,0:T(8,128)(2,1)}), bf16[64,8,769]{2,1,0:T(8,128)(2,1)S(1)}, u32[]{:S(2)}, u32[]{:S(2)}) async-start(bf16[64,8,769]{2,1,0:T(8,128)(2,1)} %pad_maximum_fusion), calls=%async_computation.4 | async-start | bytes 1835008 | tf_op jit(solution)/shard_map/all_to_all | solution.py:79
Sparse Core Ops, SparseCore 0:
  39.6 103.1 all-gather.2
  150.0 61.6 all-gather.4
